TPU v7x, 32 devices: a whole 2x2x4 slice. The times are simulated.
32 devices in a mesh: shard: 4 (over z), width: 2 (over core), unit: 4 (over y, x).
Axes of the slice: x: 2, y: 2, z: 4, core: 2. Of those that a mesh axis runs over, the one named last changes fastest.
Arguments:
- w_gate: bfloat16 [14336, 14336], P(('unit', 'shard'), 'width'), parts along dimension 0, may hold values from -0.125 to 0.125
- low_gate: bfloat16 [14336, 64], P(('unit', 'shard')), parts along dimension 0, may hold values from -0.09375 to 0.09375
- high_gate: bfloat16 [256, 14336], P('unit', 'width'), parts along dimension 0, may hold values from -0.75 to 0.75
- w_up: bfloat16 [14336, 14336], P(('unit', 'shard'), 'width'), parts along dimension 0, may hold values from -0.125 to 0.125
- low_up: bfloat16 [14336, 64], P(('unit', 'shard')), parts along dimension 0, may hold values from -0.09375 to 0.09375
- high_up: bfloat16 [256, 14336], P('unit', 'width'), parts along dimension 0, may hold values from -0.75 to 0.75
- norm_train: float32 [14336], P(('unit', 'shard', 'width')), parts along dimension 0, may hold values from 0.25 to 1.75
- norm_step: float32 [14336], P(('unit', 'shard', 'width')), parts along dimension 0, may hold values from -0.3 to 0.3
Outputs:
- serve_gate: bfloat16 [14336, 14336], P('unit', ('width', 'shard')), parts along dimension 0
- serve_up: bfloat16 [14336, 14336], P('unit', ('width', 'shard')), parts along dimension 0
- column_gate: float32 [57344], P(('unit', 'width', 'shard')), parts along dimension 0
- column_up: float32 [57344], P(('unit', 'width', 'shard')), parts along dimension 0
- serve_norm: bfloat16 [14336], P('unit'), parts along dimension 0
There are 4 independent parts, one for each index of `unit`. A program takes and returns all parts, laid end to end along the dimension named above; each array names one. Nothing has to cross between parts.
All inputs are finite; a program needn't handle non-finite values. Where the computation divides by a largest or mean magnitude, that divisor is 1e-20 or more.
Results may differ from a plain program's by a relative error of at most 0.001.
Values may be sent and summed in bfloat16 or wider, within the bound.
A program may use at most 192 MiB of HBM per device.

v0:
```python
import jax
import jax.numpy as jnp
from jax import lax
from jax.sharding import PartitionSpec as P

mix_rate = 0.5


def local(w_gate, low_gate, high_gate, w_up, low_up, high_up, norm_train, norm_step):
    fresh_gate = w_gate.astype(jnp.float32) + mix_rate * jnp.dot(
        low_gate, high_gate, preferred_element_type=jnp.float32
    )
    fresh_up = w_up.astype(jnp.float32) + mix_rate * jnp.dot(
        low_up, high_up, preferred_element_type=jnp.float32
    )
    column_gate, column_up = lax.pmax(
        (jnp.max(jnp.abs(fresh_gate), axis=0), jnp.max(jnp.abs(fresh_up), axis=0)), "shard"
    )
    narrow_gate, narrow_up = (
        (fresh_gate / column_gate).astype(jnp.bfloat16),
        (fresh_up / column_up).astype(jnp.bfloat16),
    )
    serve_gate, serve_up = (
        lax.all_to_all(narrow_gate, "shard", split_axis=1, concat_axis=0, tiled=True),
        lax.all_to_all(narrow_up, "shard", split_axis=1, concat_axis=0, tiled=True),
    )
    place = lax.axis_index("shard")
    column_gate = lax.dynamic_slice_in_dim(
        column_gate, place * serve_gate.shape[1], serve_gate.shape[1]
    )
    column_up = lax.dynamic_slice_in_dim(column_up, place * serve_up.shape[1], serve_up.shape[1])
    serve_norm = lax.all_gather(
        (norm_train + norm_step).astype(jnp.bfloat16), ("shard", "width"), axis=0, tiled=True
    )
    return (serve_gate, serve_up, column_gate, column_up, serve_norm)


def solution(mesh):
    in_specs = (
        P(("unit", "shard"), "width"),
        P(("unit", "shard"), None),
        P("unit", "width"),
        P(("unit", "shard"), "width"),
        P(("unit", "shard"), None),
        P("unit", "width"),
        P(("unit", "shard", "width")),
        P(("unit", "shard", "width")),
    )
    out_specs = (
        P("unit", ("width", "shard")),
        P("unit", ("width", "shard")),
        P(("unit", "width", "shard")),
        P(("unit", "width", "shard")),
        P("unit"),
    )
    return jax.shard_map(local, mesh=mesh, in_specs=in_specs, out_specs=out_specs, check_vma=False)
```

profile of v0, /device:TPU:16, one launch (start us, length us, event | category | flops | bytes accessed | tf_op | source)
XLA Modules:
  0.0 675.2 jit_solution(659145506202103146)
XLA Ops:
  0.6 0.0 copy-start
  0.6 0.0 copy-start.2
  0.7 0.0 copy-start.4
  0.7 0.0 copy-start.3
  0.7 1.1 copy-done
  1.8 15.2 %abs_reduce_fusion = (f32[7168]{0:T(1024)S(1)}, f32[896,7168]{1,0:T(8,128)}) fusion(bf16[896,7168]{1,0:T(8,128)(2,1)} %param.11, bf16[896,64]{0,1:T(8,128)(2,1)} %param.12, bf16[64,7168]{1,0:T(8,128)(2,1)S(1)} %copy-done), kind=kOutput, calls=%fused_computation.1 | convolution fusion | flops 854189056 | bytes 39596032 | tf_op jit(solution)/shard_map/dot_general | solution.py:13
  17.0 0.0 copy-done.2
  17.0 0.0 copy-done.4
  17.0 0.0 copy-done.3
  17.0 10.3 %abs_reduce_fusion.1 = (f32[7168]{0:T(1024)S(1)}, f32[896,7168]{1,0:T(8,128)}) fusion(bf16[896,7168]{1,0:T(8,128)(2,1)S(1)} %copy-done.2, bf16[896,64]{0,1:T(8,128)(2,1)S(1)} %copy-done.4, bf16[64,7168]{1,0:T(8,128)(2,1)S(1)} %copy-done.3), kind=kOutput, calls=%fused_computation.4 | convolution fusion | flops 854189056 | bytes 39596032 | tf_op jit(solution)/shard_map/dot_general | solution.py:10
  27.3 18.1 %all-reduce.1 = (f32[7168]{0:T(1024)S(1)}, f32[7168]{0:T(1024)S(1)}) all-reduce(f32[7168]{0:T(1024)S(1)} %get-tuple-element.7, f32[7168]{0:T(1024)S(1)} %get-tuple-element.9), channel_id=1, replica_groups=mesh['shard'=4,'width'=2,'unit'=4] {'shard'}, use_global_device_ids=true, to_apply=%region_1.0 | all-reduce | flops 14336 | bytes 114688 | tf_op jit(solution)/shard_map/pmax | solution.py:16
  45.5 29.9 %divide_convert_fusion = (bf16[896,7168]{1,0:T(8,128)(2,1)}, bf16[896,7168]{1,0:T(8,128)(2,1)S(1)}) fusion(f32[896,7168]{1,0:T(8,128)} %get-tuple-element.10, bf16[896,7168]{1,0:T(8,128)(2,1)} %param.11, f32[7168]{0:T(1024)S(1)} %get-tuple-element.6, f32[7168]{0:T(1024)S(1)} %get-tuple-element.5, f32[896,7168]{1,0:T(8,128)} %get-tuple-element.8, ...), kind=kLoop, calls=%fused_computation | loop fusion | flops 64225280 | bytes 102817792 | tf_op jit(solution)/shard_map/convert_element_type | solution.py:21
  75.4 5.1 copy.22
  80.5 8.6 %all-to-all-start = ((bf16[896,4,1792]{2,0,1:T(8,128)(2,1)}), bf16[896,4,1792]{2,0,1:T(8,128)(2,1)}, u32[]{:S(2)}, u32[]{:S(2)}) async-start(bf16[896,4,1792]{2,0,1:T(8,128)(2,1)} %bitcast.20), calls=%async_computation | async-start | bytes 25690112 | tf_op jit(solution)/shard_map/all_to_all | solution.py:24
  89.1 0.0 copy-start.7
  89.1 0.0 copy-start.5
  89.1 0.0 copy-start.6
  89.1 10.7 %copy.21 = bf16[112,4,8,1792]{3,2,0,1:T(8,128)(2,1)} copy(bf16[112,4,8,1792]{3,2,1,0:T(8,128)(2,1)} %bitcast.21) | data formatting | bytes 25690112 | tf_op jit(solution)/shard_map/all_to_all | solution.py:25
  99.8 260.9 %all-to-all-done = bf16[896,4,1792]{2,0,1:T(8,128)(2,1)} async-done(((bf16[896,4,1792]{2,0,1:T(8,128)(2,1)}), bf16[896,4,1792]{2,0,1:T(8,128)(2,1)}, u32[]{:S(2)}, u32[]{:S(2)}) %all-to-all-start) | async-done | bytes 12845088 | tf_op jit(solution)/shard_map/all_to_all | solution.py:24
  360.7 9.7 %all-to-all-start.1 = ((bf16[896,4,1792]{2,0,1:T(8,128)(2,1)}), bf16[896,4,1792]{2,0,1:T(8,128)(2,1)}, u32[]{:S(2)}, u32[]{:S(2)}) async-start(bf16[896,4,1792]{2,0,1:T(8,128)(2,1)} %bitcast.19), calls=%async_computation.1 | async-start | bytes 25690112 | tf_op jit(solution)/shard_map/all_to_all | solution.py:25
  370.4 0.7 dynamic_slice.6
  371.1 0.7 dynamic_slice.7
  371.7 0.0 copy-done.7
  371.7 0.6 dynamic-slice
  373.0 0.0 copy-done.5
  373.0 0.0 copy-done.6
  373.0 0.3 dynamic-update-slice
  373.3 280.6 %all-reduce = bf16[3584]{0:T(1024)(128)(2,1)} all-reduce(bf16[3584]{0:T(1024)(128)(2,1)S(1)} %dynamic-update-slice), channel_id=1, replica_groups=mesh['shard'=4,'width'=2,'unit'=4] {'shard','width'}, use_global_device_ids=true, to_apply=%add | all-reduce | flops 3584 | bytes 14336
  653.9 0.0 all-to-all-done.1
  653.9 0.0 copy-start.1
  653.9 10.7 %copy.26 = bf16[3584,1792]{1,0:T(8,128)(2,1)} copy(bf16[3584,1792]{1,0:T(8,128)(2,1)} %bitcast.1) | data formatting | bytes 25690112
  664.6 10.6 %copy.27 = bf16[3584,1792]{1,0:T(8,128)(2,1)} copy(bf16[3584,1792]{1,0:T(8,128)(2,1)} %bitcast.3) | data formatting | bytes 25690112
  675.2 0.0 copy-done.1
  (2 shorter events, 0.0 us)
Async XLA Ops:
  0.6 1.2 copy-start
  0.6 16.4 %copy-start.2 = (bf16[896,7168]{1,0:T(8,128)(2,1)S(1)}, bf16[896,7168]{1,0:T(8,128)(2,1)}, u32[]{:S(2)}) copy-start(bf16[896,7168]{1,0:T(8,128)(2,1)} %param.8) | copy-start | bytes 38535172
  0.7 16.4 %copy-start.4 = (bf16[896,64]{0,1:T(8,128)(2,1)S(1)}, bf16[896,64]{0,1:T(8,128)(2,1)}, u32[]{:S(2)}) copy-start(bf16[896,64]{0,1:T(8,128)(2,1)} %param.9) | copy-start | bytes 344068
  0.7 16.3 %copy-start.3 = (bf16[64,7168]{1,0:T(8,128)(2,1)S(1)}, bf16[64,7168]{1,0:T(8,128)(2,1)}, u32[]{:S(2)}) copy-start(bf16[64,7168]{1,0:T(8,128)(2,1)} %param.10) | copy-start | bytes 2752516
  80.5 280.2 %all-to-all-start = ((bf16[896,4,1792]{2,0,1:T(8,128)(2,1)}), bf16[896,4,1792]{2,0,1:T(8,128)(2,1)}, u32[]{:S(2)}, u32[]{:S(2)}) async-start(bf16[896,4,1792]{2,0,1:T(8,128)(2,1)} %bitcast.20), calls=%async_computation | async-start | bytes 25690112 | tf_op jit(solution)/shard_map/all_to_all | solution.py:24
  89.1 282.6 %copy-start.7 = (u32[32]{0:T(128)S(1)}, u32[32]{0:T(128)}, u32[]{:S(2)}) copy-start(u32[32]{0:T(128)} %constant.17) | copy-start | bytes 388
  89.1 283.9 %copy-start.5 = (f32[448]{0:T(512)S(1)}, f32[448]{0:T(512)}, u32[]{:S(2)}) copy-start(f32[448]{0:T(512)} %param.14) | copy-start | bytes 5380
  89.1 283.9 %copy-start.6 = (f32[448]{0:T(512)S(1)}, f32[448]{0:T(512)}, u32[]{:S(2)}) copy-start(f32[448]{0:T(512)} %param.15) | copy-start | bytes 5380
  360.7 293.2 %all-to-all-start.1 = ((bf16[896,4,1792]{2,0,1:T(8,128)(2,1)}), bf16[896,4,1792]{2,0,1:T(8,128)(2,1)}, u32[]{:S(2)}, u32[]{:S(2)}) async-start(bf16[896,4,1792]{2,0,1:T(8,128)(2,1)} %bitcast.19), calls=%async_computation.1 | async-start | bytes 25690112 | tf_op jit(solution)/shard_map/all_to_all | solution.py:25
  653.9 21.3 %copy-start.1 = (bf16[64,7168]{1,0:T(8,128)(2,1)S(1)}, bf16[64,7168]{1,0:T(8,128)(2,1)}, u32[]{:S(2)}) copy-start(bf16[64,7168]{1,0:T(8,128)(2,1)} %param.13) | copy-start | bytes 2752516
where the time goes:
time: 676 us; the launch traced here: 675 us
  blocking collectives  299 us (44%)
  waiting for transfers between devices  261 us (39%)
  local copies, waits for them, and re-layouts  40.5 us (6%)
  other arithmetic  29.9 us (4%)
  matrix products  25.5 us (4%)
  starting transfers between devices  18.3 us (3%)
    unnamed x1, blocking collectives  281 us
    all_to_all x1, waiting for transfers between devices, local(): lax.all_to_all(narrow_gate, 'shard', split_axis=1, concat_axis=0, tiled=T...  261 us
    convert_element_type x1, other arithmetic, local(): (fresh_up / column_up).astype(jnp.bfloat16)  29.9 us
    unnamed x21, local copies, waits for them, and re-layouts  23.3 us
    pmax x1, blocking collectives, local(): lax.pmax((jnp.max(jnp.abs(fresh_gate), axis=0), jnp.max(jnp.abs(fresh_up)...  18.1 us
    dot_general x1, matrix products, local(): jnp.dot(low_up, high_up, preferred_element_type=jnp.float32)  15.2 us
  transfers between devices with their start and end apart: 2, of which 1 were waited for; matrix products, arithmetic and copies ran while one was open for 2% of the time, Pallas kernels for 0%

commit v1 on v0

--- a/solution.py
+++ b/solution.py
@@ -1,12 +1,17 @@
+import functools
+
 import jax
 import jax.numpy as jnp
 from jax import lax
+from jax.experimental import pallas as pl
+from jax.experimental.pallas import tpu as pltpu
 from jax.sharding import PartitionSpec as P
 
 mix_rate = 0.5
-
-
-def local(w_gate, low_gate, high_gate, w_up, low_up, high_up, norm_train, norm_step):
+CHUNK = 256
+
+
+def local_plain(w_gate, low_gate, high_gate, w_up, low_up, high_up, norm_train, norm_step):
     fresh_gate = w_gate.astype(jnp.float32) + mix_rate * jnp.dot(
         low_gate, high_gate, preferred_element_type=jnp.float32
     )
@@ -33,6 +38,240 @@
         (norm_train + norm_step).astype(jnp.bfloat16), ("shard", "width"), axis=0, tiled=True
     )
     return (serve_gate, serve_up, column_gate, column_up, serve_norm)
+
+
+def exchange(
+    n, nw, chunks, w_gate, w_up, low, high_gate, high_up, norm,
+    out_gate, out_up, col_gate, col_up, norm_all,
+    low_all, mix_gate, mix_up, fresh,
+    send, recv, low_send, low_recv, fwd_send, fwd_recv, norm_send, norm_recv, own,
+):
+    me = lax.axis_index("shard")
+    side = lax.axis_index("width")
+    rows = w_gate.shape[0]
+    cols = out_gate.shape[1]
+    rank = high_gate.shape[0]
+    half = rows // nw
+    ws = (w_gate, w_up)
+    outs = (out_gate, out_up)
+    cuts = [(at, min(CHUNK, cols - at)) for at in range(0, cols, CHUNK)]
+    others = [(a, b) for a in range(n) for b in range(nw) if (a, b) != (0, 0)]
+
+    def peer(a, b):
+        return {"shard": lax.rem(me + a, n), "width": lax.rem(side + b, nw)}
+
+    barrier = pltpu.get_barrier_semaphore()
+    for a, b in others:
+        pl.semaphore_signal(
+            barrier, inc=1, device_id=peer(a, b), device_id_type=pl.DeviceIdType.MESH
+        )
+    pl.semaphore_wait(barrier, len(others))
+
+    def low_part(s, h):
+        return pl.ds(pl.multiple_of(s * rows + h * half, 16), half)
+
+    def low_copy(dst, s):
+        return pltpu.make_async_remote_copy(
+            src_ref=low.at[pl.ds(pl.multiple_of(side * half, 16), half)],
+            dst_ref=low_all.at[low_part(s, side)],
+            send_sem=low_send.at[dst], recv_sem=low_recv.at[s],
+            device_id={"shard": dst, "width": side}, device_id_type=pl.DeviceIdType.MESH,
+        )
+
+    def low_forward(s, h, b):
+        return pltpu.make_async_remote_copy(
+            src_ref=low_all.at[low_part(s, h)], dst_ref=low_all.at[low_part(s, h)],
+            send_sem=fwd_send.at[s, b], recv_sem=fwd_recv.at[s, b],
+            device_id={"shard": me, "width": lax.rem(side + b, nw)},
+            device_id_type=pl.DeviceIdType.MESH,
+        )
+
+    def piece(k, c, dst, s):
+        at, wide = cuts[c]
+        return pltpu.make_async_remote_copy(
+            src_ref=ws[k].at[:, pl.ds(pl.multiple_of(dst * cols + at, 128), wide)],
+            dst_ref=outs[k].at[pl.ds(pl.multiple_of(s * rows, 16), rows), pl.ds(at, wide)],
+            send_sem=send.at[dst, k, c], recv_sem=recv.at[s, k, c],
+            device_id={"shard": dst, "width": side}, device_id_type=pl.DeviceIdType.MESH,
+        )
+
+    def norm_copy(i, a, b, slot):
+        return pltpu.make_async_remote_copy(
+            src_ref=norm, dst_ref=norm_all.at[slot],
+            send_sem=norm_send.at[i], recv_sem=norm_recv.at[i],
+            device_id=peer(a, b), device_id_type=pl.DeviceIdType.MESH,
+        )
+
+    for d in range(1, n):
+        for sign in (1, -1):
+            dst = me + sign * d
+
+            @pl.when((dst >= 0) & (dst < n))
+            def _(dst=dst):
+                low_copy(dst, me).start()
+
+    slot = me * nw + side
+    for i, (a, b) in enumerate(others):
+        norm_copy(i, a, b, slot).start()
+
+    for d in range(1, n):
+        for k in range(2):
+            for c in range(chunks):
+                for sign in (1, -1):
+                    dst = me + sign * d
+
+                    @pl.when((dst >= 0) & (dst < n))
+                    def _(dst=dst, k=k, c=c):
+                        piece(k, c, dst, me).start()
+
+    mine = pl.ds(pl.multiple_of(me * rows, 16), rows)
+    my_cols = pl.ds(pl.multiple_of(me * cols, 128), cols)
+    local = [
+        pltpu.make_async_copy(w_gate.at[:, my_cols], out_gate.at[mine], own.at[0]),
+        pltpu.make_async_copy(w_up.at[:, my_cols], out_up.at[mine], own.at[1]),
+        pltpu.make_async_copy(low, low_all.at[mine], own.at[2]),
+        pltpu.make_async_copy(high_gate.at[:, my_cols], mix_gate.at[pl.ds(0, rank)], own.at[3]),
+        pltpu.make_async_copy(high_up.at[:, my_cols], mix_up.at[pl.ds(rank, rank)], own.at[4]),
+        pltpu.make_async_copy(norm, norm_all.at[slot], own.at[5]),
+    ]
+    for copy in local:
+        copy.start()
+    mix_gate[rank:, :] = jnp.zeros((rank, cols), mix_gate.dtype)
+    mix_up[:rank, :] = jnp.zeros((rank, cols), mix_up.dtype)
+
+    for d in range(1, n):
+        for sign in (1, -1):
+            src = me + sign * d
+
+            @pl.when((src >= 0) & (src < n))
+            def _(src=src):
+                low_copy(src, src).wait_recv()
+                for b in range(1, nw):
+                    low_forward(src, side, b).start()
+
+    for copy in local:
+        copy.wait()
+    for d in range(1, n):
+        for sign in (1, -1):
+            src = me + sign * d
+
+            @pl.when((src >= 0) & (src < n))
+            def _(src=src):
+                for b in range(1, nw):
+                    low_forward(src, lax.rem(side + nw - b, nw), b).wait_recv()
+
+    step = rows // 2
+    for k, (out, mix, col) in enumerate(((out_gate, mix_gate, col_gate), (out_up, mix_up, col_up))):
+        for c, (at, wide) in enumerate(cuts):
+            for s in range(n):
+
+                @pl.when(s != me)
+                def _(s=s):
+                    piece(k, c, s, s).wait_recv()
+
+            here = pl.ds(at, wide)
+            span = pl.ds(0, wide)
+
+            def build(i, top):
+                r = pl.ds(pl.multiple_of(i * step, 16), step)
+                new = out[r, here].astype(jnp.float32) + mix_rate * jnp.dot(
+                    low_all[r, :], mix[:, here], preferred_element_type=jnp.float32
+                )
+                fresh[r, span] = new
+                return jnp.maximum(top, jnp.max(jnp.abs(new), axis=0, keepdims=True))
+
+            top = lax.fori_loop(0, n * rows // step, build, jnp.zeros((1, wide), jnp.float32))
+            col[:, here] = top
+            inverse = 1.0 / top
+
+            def scale(i, _):
+                r = pl.ds(pl.multiple_of(i * step, 16), step)
+                out[r, here] = (fresh[r, span] * inverse).astype(out.dtype)
+                return 0
+
+            lax.fori_loop(0, n * rows // step, scale, 0)
+
+    for d in range(1, n):
+        for sign in (1, -1):
+            dst = me + sign * d
+
+            @pl.when((dst >= 0) & (dst < n))
+            def _(dst=dst):
+                low_copy(dst, me).wait_send()
+                for k in range(2):
+                    for c in range(chunks):
+                        piece(k, c, dst, me).wait_send()
+                for b in range(1, nw):
+                    low_forward(dst, side, b).wait_send()
+    for i, (a, b) in enumerate(others):
+        norm_copy(i, a, b, slot).wait()
+
+
+def write_out(parts, gate, up, out_gate, out_up, sems):
+    rows = gate.shape[0] // parts
+    copies = [
+        pltpu.make_async_copy(x.at[pl.ds(i * rows, rows)], y.at[pl.ds(i * rows, rows)], sems.at[k, i])
+        for k, (x, y) in enumerate(((gate, out_gate), (up, out_up)))
+        for i in range(parts)
+    ]
+    for copy in copies:
+        copy.start()
+    for copy in copies:
+        copy.wait()
+
+
+def local_kernel(n, nw, w_gate, low_gate, high_gate, w_up, low_up, high_up, norm_train, norm_step):
+    rows = w_gate.shape[0]
+    cols = w_gate.shape[1] // n
+    rank = low_gate.shape[1]
+    chunks = pl.cdiv(cols, CHUNK)
+    size = norm_train.shape[0]
+    low = jnp.concatenate([low_gate, low_up], axis=1)
+    padded = pl.cdiv(size, 128) * 128
+    norm = jnp.broadcast_to(jnp.pad(norm_train + norm_step, (0, padded - size))[None], (8, padded))
+    hbm = pl.BlockSpec(memory_space=pl.ANY)
+    vmem = pl.BlockSpec(memory_space=pltpu.VMEM)
+    dma = pltpu.SemaphoreType.DMA
+    gate, up, col_gate, col_up, norm_all = pl.pallas_call(
+        functools.partial(exchange, n, nw, chunks),
+        out_shape=(
+            pltpu.VMEM((n * rows, cols), jnp.bfloat16),
+            pltpu.VMEM((n * rows, cols), jnp.bfloat16),
+            jax.ShapeDtypeStruct((1, cols), jnp.float32),
+            jax.ShapeDtypeStruct((1, cols), jnp.float32),
+            jax.ShapeDtypeStruct((n * nw, 8, padded), jnp.float32),
+        ),
+        in_specs=[hbm] * 6,
+        out_specs=(vmem, vmem, vmem, vmem, hbm),
+        scratch_shapes=[
+            pltpu.VMEM((n * rows, 2 * rank), jnp.bfloat16),
+            pltpu.VMEM((2 * rank, cols), jnp.bfloat16),
+            pltpu.VMEM((2 * rank, cols), jnp.bfloat16),
+            pltpu.VMEM((n * rows, CHUNK), jnp.float32),
+            dma((n, 2, chunks)), dma((n, 2, chunks)),
+            dma((n,)), dma((n,)),
+            dma((n, nw)), dma((n, nw)),
+            dma((n * nw,)), dma((n * nw,)),
+            dma((6,)),
+        ],
+        compiler_params=pltpu.CompilerParams(
+            collective_id=0, has_side_effects=True, vmem_limit_bytes=24 * 1024 * 1024
+        ),
+    )(w_gate, w_up, low, high_gate, high_up, norm)
+    parts = 4
+    serve_gate, serve_up = pl.pallas_call(
+        functools.partial(write_out, parts),
+        out_shape=(
+            jax.ShapeDtypeStruct((n * rows, cols), jnp.bfloat16),
+            jax.ShapeDtypeStruct((n * rows, cols), jnp.bfloat16),
+        ),
+        in_specs=[hbm, hbm],
+        out_specs=(hbm, hbm),
+        scratch_shapes=[dma((2, parts))],
+        compiler_params=pltpu.CompilerParams(vmem_limit_bytes=8 * 1024 * 1024),
+    )(gate, up)
+    serve_norm = norm_all[:, 0, :size].reshape(-1).astype(jnp.bfloat16)
+    return serve_gate, serve_up, col_gate[0], col_up[0], serve_norm
 
 
 def solution(mesh):
@@ -53,4 +292,17 @@
         P(("unit", "width", "shard")),
         P("unit"),
     )
+    n, nw = mesh.shape["shard"], mesh.shape["width"]
+
+    def local(*args):
+        rows, cols = args[0].shape[0], args[0].shape[1] // n
+        fits = (
+            args[0].shape[1] % n == 0
+            and cols % 128 == 0
+            and rows % (16 * nw) == 0
+            and n * rows * cols * 4 <= 32 * 2**20
+            and 2 * args[1].shape[1] % 128 == 0
+        )
+        return local_kernel(n, nw, *args) if fits else local_plain(*args)
+
     return jax.shard_map(local, mesh=mesh, in_specs=in_specs, out_specs=out_specs, check_vma=False)

time: 676 us -> 590 us (0.87)
  Pallas kernels: 0 us -> 576 us
  blocking collectives: 299 us -> 0 us
  waiting for transfers between devices: 261 us -> 0 us
  local copies, waits for them, and re-layouts: 40.5 us -> 5.22 us
  other arithmetic: 29.9 us -> 2.08 us
  matrix products: 25.5 us -> 0 us
  starting transfers between devices: 18.3 us -> 0 us
    pallas_call x0 -> x2, Pallas kernels: none -> 576 us  [the longest x1 567 us: local_kernel(): pl.pallas_call(functools.partial(exchange, n, nw, chunks), out_shape=(plt...]
    unnamed x1 -> x0, blocking collectives: 281 us -> none
    all_to_all x2 -> x0, waiting for transfers between devices: 261 us -> none  [the longest x1 261 us: local(): lax.all_to_all(narrow_gate, 'shard', split_axis=1, concat_axis=0, tiled=T...]
    convert_element_type x2 -> x0, other arithmetic: 29.9 us -> none  [the longest x1 29.9 us: local(): (fresh_up / column_up).astype(jnp.bfloat16)]
    dot_general x2 -> x0, matrix products: 25.5 us -> none  [the longest x1 15.2 us: local(): jnp.dot(low_up, high_up, preferred_element_type=jnp.float32)]
    unnamed x21 -> x6, local copies, waits for them, and re-layouts: 23.3 us -> 4.48 us
    all_to_all x2 -> x0, starting transfers between devices: 18.3 us -> none  [the longest x1 9.69 us: local(): lax.all_to_all(narrow_up, 'shard', split_axis=1, concat_axis=0, tiled=True)]
    pmax x1 -> x0, blocking collectives: 18.1 us -> none  [local(): lax.pmax((jnp.max(jnp.abs(fresh_gate), axis=0), jnp.max(jnp.abs(fresh_up)...]
  transfers between devices with their start and end apart: 2 -> 0, of which waited for: 1 -> 0; matrix products, arithmetic and copies ran while one was open for 2% -> 0% of each run, Pallas kernels for 0% -> 0%
where the time goes in v1:
time: 590 us; the launch traced here: 584 us
  Pallas kernels  576 us (98%)
    pallas_call x1, Pallas kernels, local_kernel(): pl.pallas_call(functools.partial(exchange, n, nw, chunks), out_shape=(plt...  567 us

profile of v1, /device:TPU:16, one launch (start us, length us, event | category | flops | bytes accessed | tf_op | source)
XLA Modules:
  0.0 583.5 jit_solution(14777755477755946647)
XLA Ops:
  0.6 0.7 add.5
  1.3 1.1 copy.15
  2.4 1.1 copy.16
  3.5 0.1 pad_maximum_fusion.low
  3.6 0.0 copy-start
  3.6 1.2 copy-done
  4.8 0.0 copy-start.1
  4.8 1.2 copy-done.1
  6.0 566.8 %shard_map.119 = (bf16[3584,1792]{1,0:T(8,128)(2,1)S(1)}, bf16[3584,1792]{1,0:T(8,128)(2,1)S(1)}, f32[1,1792]{1,0:T(1,128)S(1)}, f32[1,1792]{1,0:T(1,128)S(1)}, f32[8,8,512]{2,1,0:T(8,128)S(1)}) custom-call(bf16[896,7168]{1,0:T(8,128)(2,1)} %w_gate.1, bf16[896,7168]{1,0:T(8,128)(2,1)} %w_up.1, bf16[896,128]{1,0:T(8,128)(2,1)S(1)} %pad_maximum_fusion.low, ...), custom_call_target="tpu_custom_call" | custom-call | tf_op jit(solution)/shard_map/pallas_call | solution.py:235
  572.8 8.7 %shard_map.120 = (bf16[3584,1792]{1,0:T(8,128)(2,1)}, bf16[3584,1792]{1,0:T(8,128)(2,1)}) custom-call(bf16[3584,1792]{1,0:T(8,128)(2,1)S(1)} %get-tuple-element.12.gate, bf16[3584,1792]{1,0:T(8,128)(2,1)S(1)} %get-tuple-element.13.up), custom_call_target="tpu_custom_call" | custom-call | tf_op jit(solution)/shard_map/pallas_call | solution.py:262
  581.6 0.6 reduce
  582.2 0.6 reduce.1
  582.8 0.7 convert_element_type.6
  (3 shorter events, 0.1 us)
Async XLA Ops:
  3.6 1.2 copy-start
  4.8 1.2 copy-start.1
